TPU v7x, 8 devices: a whole 2x2x1 slice. The times are simulated.
8 devices in a mesh: sys: 1 (over z), seg: 8 (over y, x, core).
Axes of the slice: x: 2, y: 2, z: 1, core: 2. Of those that a mesh axis runs over, the one named last changes fastest.
Arguments:
- positions: bfloat16 [16384, 320], P(('sys', 'seg'))
- charges: float32 [16384], P(('sys', 'seg'))
- pair_band: int32 [8, 7], P(('sys', 'seg'))
Outputs:
- output 1: float32 [16384, 320], P(('sys', 'seg'))
- output 2: float32 [1], P('sys')
All inputs are finite; a program needn't handle non-finite values.
Results may differ from a plain program's by a relative error of at most 0.001.
Values are sent between devices in bfloat16 or wider.
A program may use at most 1 GiB of HBM per device.

v0:
```python
import jax
import jax.numpy as jnp
from jax import lax
from jax.sharding import PartitionSpec as P


def solution(mesh):
    seg_len = mesh.shape['seg']
    fwd_perm = [(src_dev, (src_dev + 1) % seg_len) for src_dev in range(seg_len)]

    def device_fn(positions, charges, pair_band):
        n_rows, feat_dim = positions.shape
        reach_steps = (pair_band.shape[1] - 1) // 2
        inv_lsq = 1.0 / feat_dim
        band_row = pair_band[0]
        row_ids = jnp.arange(n_rows)
        host_sq = jnp.einsum('nd,nd->n', positions, positions, preferred_element_type=jnp.float32)

        def pair_weights(x_vis, q_vis, sq_vis):
            cross_dot = jnp.einsum('id,jd->ij', positions, x_vis, preferred_element_type=jnp.float32)
            sq_dist = jnp.maximum(host_sq[:, None] + sq_vis[None, :] - 2.0 * cross_dot, 0.0)
            return charges[:, None] * q_vis[None, :] * jnp.exp(sq_dist * (-0.5 * inv_lsq))

        self_w = jnp.where(row_ids[:, None] == row_ids[None, :], 0.0, pair_weights(positions, charges, host_sq))
        self_pull = jnp.dot(self_w.astype(jnp.bfloat16), positions, preferred_element_type=jnp.float32)
        forces = (jnp.sum(self_w, axis=1)[:, None] * positions - self_pull) * inv_lsq
        energy = 0.5 * jnp.sum(self_w)

        def live_pair(operands):
            x_vis, q_vis = operands
            sq_vis = jnp.einsum('nd,nd->n', x_vis, x_vis, preferred_element_type=jnp.float32)
            weights = pair_weights(x_vis, q_vis, sq_vis)
            w_low = weights.astype(jnp.bfloat16)
            host_pull = jnp.dot(w_low, x_vis, preferred_element_type=jnp.float32)
            vis_pull = jnp.einsum('ij,id->jd', w_low, positions, preferred_element_type=jnp.float32)
            host_part = (jnp.sum(weights, axis=1)[:, None] * positions - host_pull) * inv_lsq
            vis_part = (jnp.sum(weights, axis=0)[:, None] * x_vis - vis_pull) * inv_lsq
            return host_part, vis_part, jnp.sum(weights)

        def dead_pair(operands):
            zero_rows = jnp.zeros((n_rows, feat_dim), jnp.float32)
            return zero_rows, zero_rows, jnp.zeros((), jnp.float32)

        x_vis, q_vis = positions, charges
        react_acc = jnp.zeros((n_rows, feat_dim), jnp.float32)
        for step_idx in range(1, reach_steps + 1):
            x_vis = lax.ppermute(x_vis, 'seg', fwd_perm)
            q_vis = lax.ppermute(q_vis, 'seg', fwd_perm)
            if step_idx > 1:
                react_acc = lax.ppermute(react_acc, 'seg', fwd_perm)
            host_part, vis_part, pair_energy = lax.cond(band_row[reach_steps - step_idx] != 0, live_pair, dead_pair, (x_vis, q_vis))
            forces = forces + host_part
            react_acc = react_acc + vis_part
            energy = energy + pair_energy
        back_perm = [(src_dev, (src_dev - reach_steps) % seg_len) for src_dev in range(seg_len)]
        forces = forces + lax.ppermute(react_acc, 'seg', back_perm)
        energy = lax.psum(energy, 'seg')
        return forces, energy.reshape(1)

    row_spec = P(('sys', 'seg'), None)
    vec_spec = P(('sys', 'seg'))
    return jax.shard_map(device_fn, mesh=mesh, in_specs=(row_spec, vec_spec, row_spec), out_specs=(row_spec, P('sys')), check_vma=False)
```

profile of v0, /device:TPU:0, one launch (start us, length us, event | category | flops | bytes accessed | tf_op | source)
XLA Modules:
  0.0 274.6 jit_solution(16379827345428794857)
XLA Ops:
  0.6 0.9 collective-permute-start.1
  1.5 2.6 collective-permute-start
  4.1 1.6 fusion.59
  5.7 1.4 fusion.64
  7.7 12.0 %collective-permute-done = f32[2048]{0:T(1024)S(1)} collective-permute-done((f32[2048]{0:T(1024)}, f32[2048]{0:T(1024)S(1)}, u32[]{:S(2)}, u32[]{:S(2)}) %collective-permute-start) | collective-permute-done | bytes 8224 | tf_op jit(solution)/shard_map/ppermute | solution.py:48
  19.8 0.0 collective-permute-done.1
  19.8 23.4 %conditional.3 = (f32[2048,320]{0,1:T(8,128)}, f32[2048,320]{0,1:T(8,128)}, f32[]{:T(128)}) conditional(s32[]{:T(128)} %bitcast, () %tuple.32, (f32[2048]{0:T(1024)}, f32[2048]{0:T(1024)S(1)}, f32[2048]{0:T(1024)S(1)}, bf16[2048,320]{0,1:T(8,128)(2,1)S(1)}, bf16[2048,320]{0,1:T(8,128)(2,1)}) %tuple.33), branch_computations={%region_1.2_spmd, %region_2.6_spmd} | conditional | flops 8106403840 | bytes 44900408 | solution.py:51
  19.8 0.3 fusion.16
  20.1 0.0 copy-start.4
  20.1 13.4 %fusion.60 = (f32[]{:T(128)}, f32[2048]{0:T(1024)S(1)}, f32[2048]{0:T(1024)S(1)}, bf16[2048,2048]{1,0:T(8,128)(2,1)S(1)}) fusion(bf16[2048,320]{0,1:T(8,128)(2,1)} %get-tuple-element.34, bf16[2048,320]{0,1:T(8,128)(2,1)S(1)} %get-tuple-element.33, f32[2048]{0:T(1024)S(1)} %fusion.16, f32[2048]{0:T(1024)S(1)} %get-tuple-element.32, ...), kind=kOutput, calls=%fused_computation.46 | convolution fusion | flops 2730487808 | bytes 11059204 | tf_op jit(solution)/shard_map/cond/branch_1_fun/id,jd->ij/dot_general | solution.py:20
  33.5 0.0 copy-done.4
  33.5 4.6 %fusion.13 = f32[2048,320]{0,1:T(8,128)} fusion(bf16[2048,320]{0,1:T(8,128)(2,1)S(1)} %copy-done.4, bf16[2048,2048]{1,0:T(8,128)(2,1)S(1)} %get-tuple-element.76, bf16[2048,320]{0,1:T(8,128)(2,1)S(1)} %get-tuple-element.33, f32[2048]{0:T(1024)S(1)} %get-tuple-element.66), kind=kOutput, calls=%fused_computation.10 | convolution fusion | flops 2686976000 | bytes 13639680 | tf_op jit(solution)/shard_map/cond/branch_1_fun/ij,id->jd/dot_general | solution.py:35
  38.0 4.5 %fusion.7 = f32[2048,320]{0,1:T(8,128)} fusion(bf16[2048,320]{0,1:T(8,128)(2,1)S(1)} %get-tuple-element.33, bf16[2048,2048]{1,0:T(8,128)(2,1)S(1)} %get-tuple-element.76, bf16[2048,320]{0,1:T(8,128)(2,1)S(1)} %copy-done.4, f32[2048]{0:T(1024)S(1)} %get-tuple-element.67), kind=kOutput, calls=%fused_computation.8 | convolution fusion | flops 2686976000 | bytes 13639680 | tf_op jit(solution)/shard_map/cond/branch_1_fun/dot_general | solution.py:34
  43.1 0.0 collective-permute-start.6
  43.2 1.4 collective-permute-start.3
  44.6 0.0 collective-permute-start.2
  45.3 44.0 %collective-permute-done.2 = f32[2048]{0:T(1024)S(1)} collective-permute-done((f32[2048]{0:T(1024)S(1)}, f32[2048]{0:T(1024)S(1)}, u32[]{:S(2)}, u32[]{:S(2)}) %collective-permute-start.2) | collective-permute-done | bytes 8224 | tf_op jit(solution)/shard_map/ppermute | solution.py:48
  89.3 0.0 collective-permute-done.3
  89.3 24.7 %conditional.4 = (f32[2048,320]{0,1:T(8,128)S(1)}, f32[2048,320]{0,1:T(8,128)S(1)}, f32[]{:T(128)}) conditional(s32[]{:T(128)} %bitcast.1, () %tuple.34, (f32[2048]{0:T(1024)}, f32[2048]{0:T(1024)S(1)}, f32[2048]{0:T(1024)S(1)}, bf16[2048,320]{0,1:T(8,128)(2,1)}, bf16[2048,320]{0,1:T(8,128)(2,1)}) %tuple.35), branch_computations={%region_6.0_spmd, %region_7.11_spmd} | conditional | flops 8106403840 | bytes 44900408 | solution.py:51
  89.4 1.6 fusion.33
  91.0 13.7 %fusion.61 = (f32[]{:T(128)}, f32[2048]{0:T(1024)S(1)}, f32[2048]{0:T(1024)S(1)}, bf16[2048,2048]{1,0:T(8,128)(2,1)S(1)}) fusion(bf16[2048,320]{0,1:T(8,128)(2,1)} %get-tuple-element.39, bf16[2048,320]{0,1:T(8,128)(2,1)} %get-tuple-element.38, f32[2048]{0:T(1024)S(1)} %fusion.33, f32[2048]{0:T(1024)S(1)} %get-tuple-element.37, ...), kind=kOutput, calls=%fused_computation.47 | convolution fusion | flops 2730487808 | bytes 11059204 | tf_op jit(solution)/shard_map/cond/branch_1_fun/id,jd->ij/dot_general | solution.py:20
  104.8 0.0 copy-done.5
  104.8 4.3 %fusion.30 = f32[2048,320]{0,1:T(8,128)S(1)} fusion(bf16[2048,320]{0,1:T(8,128)(2,1)S(1)} %copy-done.5, bf16[2048,2048]{1,0:T(8,128)(2,1)S(1)} %get-tuple-element.77, bf16[2048,320]{0,1:T(8,128)(2,1)} %get-tuple-element.38, f32[2048]{0:T(1024)S(1)} %get-tuple-element.69), kind=kOutput, calls=%fused_computation.22 | convolution fusion | flops 2686976000 | bytes 13639680 | tf_op jit(solution)/shard_map/cond/branch_1_fun/ij,id->jd/dot_general | solution.py:35
  109.1 4.4 %fusion.24 = f32[2048,320]{0,1:T(8,128)S(1)} fusion(bf16[2048,320]{0,1:T(8,128)(2,1)} %get-tuple-element.38, bf16[2048,2048]{1,0:T(8,128)(2,1)S(1)} %get-tuple-element.77, bf16[2048,320]{0,1:T(8,128)(2,1)S(1)} %copy-done.5, f32[2048]{0:T(1024)S(1)} %get-tuple-element.70), kind=kOutput, calls=%fused_computation.20 | convolution fusion | flops 2686976000 | bytes 13639680 | tf_op jit(solution)/shard_map/cond/branch_1_fun/dot_general | solution.py:34
  114.0 0.0 copy-start
  114.0 0.0 collective-permute-done.6
  114.0 0.0 copy-start.7
  114.1 4.6 %add.87 = f32[2048,320]{0,1:T(8,128)} add(f32[2048,320]{0,1:T(8,128)} %collective-permute-done.6, f32[2048,320]{0,1:T(8,128)S(1)} %get-tuple-element.60) | non-fusion elementwise | flops 655360 | bytes 7864320 | tf_op jit(solution)/shard_map/add | solution.py:53
  118.6 0.0 copy-done
  118.6 0.0 collective-permute-start.7
  118.6 0.6 collective-permute-start.5
  119.2 0.0 collective-permute-start.4
  119.9 44.9 %collective-permute-done.4 = f32[2048]{0:T(1024)S(1)} collective-permute-done((f32[2048]{0:T(1024)S(1)}, f32[2048]{0:T(1024)S(1)}, u32[]{:S(2)}, u32[]{:S(2)}) %collective-permute-start.4) | collective-permute-done | bytes 8224 | tf_op jit(solution)/shard_map/ppermute | solution.py:48
  164.8 0.0 collective-permute-done.5
  164.8 0.0 copy-done.7
  164.8 6.7 %conditional.5 = (f32[2048,320]{0,1:T(8,128)S(1)}, f32[2048,320]{0,1:T(8,128)S(1)}, f32[]{:T(128)}) conditional(s32[]{:T(128)} %bitcast.2, () %tuple.36, (f32[2048]{0:T(1024)S(1)}, f32[2048]{0:T(1024)S(1)}, f32[2048]{0:T(1024)S(1)}, bf16[2048,320]{0,1:T(8,128)(2,1)}, bf16[2048,320]{0,1:T(8,128)(2,1)}) %tuple.62), branch_computations={%region_11.0_spmd, %region_12.16_spmd} | conditional | flops 8106403840 | bytes 44900408 | solution.py:51
  164.8 0.3 broadcast.70
  165.1 0.3 broadcast.70.clone
  171.4 0.0 copy-start.2
  171.5 0.0 collective-permute-done.7
  171.5 0.0 copy-start.3
  171.5 4.6 %add.88 = f32[2048,320]{0,1:T(8,128)} add(f32[2048,320]{0,1:T(8,128)} %collective-permute-done.7, f32[2048,320]{0,1:T(8,128)S(1)} %get-tuple-element.61) | non-fusion elementwise | flops 655360 | bytes 7864320 | tf_op jit(solution)/shard_map/add | solution.py:53
  176.1 0.0 collective-permute-start.8
  176.1 14.8 %fusion.63 = (f32[]{:T(128)}, f32[2048]{0:T(1024)S(1)}, bf16[2048,2048]{0,1:T(8,128)(2,1)}) fusion(bf16[2048,320]{0,1:T(8,128)(2,1)S(1)} %copy-done.3, f32[2048]{0:T(1024)S(1)} %fusion.59, f32[2048]{0:T(1024)S(1)} %copy-done.7), kind=kOutput, calls=%fused_computation.49 | convolution fusion | flops 2734684160 | bytes 9723908 | tf_op jit(solution)/shard_map/id,jd->ij/dot_general | solution.py:20
  191.6 8.6 %fusion.56 = f32[2048,320]{0,1:T(8,128)} fusion(bf16[2048,320]{0,1:T(8,128)(2,1)} %param.9, bf16[2048,2048]{0,1:T(8,128)(2,1)} %get-tuple-element.82, f32[2048]{0:T(1024)S(1)} %get-tuple-element.75), kind=kOutput, calls=%fused_computation.43 | convolution fusion | flops 2686976000 | bytes 12328960 | tf_op jit(solution)/shard_map/dot_general | solution.py:25
  200.2 67.0 %psum.7 = f32[1]{0:T(128)} all-reduce(f32[1]{0:T(128)} %bitcast.3), channel_id=1, replica_groups=mesh['sys'=1,'seg'=8] {'seg'}, use_global_device_ids=true, to_apply=%region_17.18 | all-reduce | flops 1 | bytes 8 | tf_op jit(solution)/shard_map/psum | solution.py:57
  267.2 0.0 collective-permute-done.8
  267.2 7.0 %add_add_fusion = f32[2048,320]{0,1:T(8,128)} fusion(f32[2048,320]{0,1:T(8,128)} %collective-permute-done.8, f32[2048,320]{0,1:T(8,128)} %copy-done.2, f32[2048,320]{0,1:T(8,128)S(1)} %copy-done.1, f32[2048,320]{0,1:T(8,128)} %fusion.56, f32[2048,320]{0,1:T(8,128)} %get-tuple-element.56), kind=kLoop, calls=%fused_computation.45 | loop fusion | flops 2621440 | bytes 15728640 | tf_op jit(solution)/shard_map/add | solution.py:56
  (5 shorter events, 0.0 us)
Async XLA Ops:
  0.6 19.1 %collective-permute-start.1 = (bf16[2048,320]{0,1:T(8,128)(2,1)}, bf16[2048,320]{0,1:T(8,128)(2,1)S(1)}, u32[]{:S(2)}, u32[]{:S(2)}) collective-permute-start(bf16[2048,320]{0,1:T(8,128)(2,1)} %param.9), channel_id=1, source_target_pairs={{0,1},{1,2},{2,3},{3,4},{4,5},{5,6},{6,7},{7,0}} | collective-permute-start | bytes 3932168 | tf_op jit(solution)/shard_map/ppermute | solution.py:47
  1.5 18.3 %collective-permute-start = (f32[2048]{0:T(1024)}, f32[2048]{0:T(1024)S(1)}, u32[]{:S(2)}, u32[]{:S(2)}) collective-permute-start(f32[2048]{0:T(1024)} %param.10), channel_id=1, source_target_pairs={{0,1},{1,2},{2,3},{3,4},{4,5},{5,6},{6,7},{7,0}} | collective-permute-start | bytes 24584 | tf_op jit(solution)/shard_map/ppermute | solution.py:48
  20.1 13.4 %copy-start.4 = (bf16[2048,320]{0,1:T(8,128)(2,1)S(1)}, bf16[2048,320]{0,1:T(8,128)(2,1)}, u32[]{:S(2)}) copy-start(bf16[2048,320]{0,1:T(8,128)(2,1)} %get-tuple-element.34) | copy-start | bytes 3932164 | tf_op jit(solution)/shard_map/cond
  43.1 70.9 %collective-permute-start.6 = (f32[2048,320]{0,1:T(8,128)}, f32[2048,320]{0,1:T(8,128)}, u32[]{:S(2)}, u32[]{:S(2)}) collective-permute-start(f32[2048,320]{0,1:T(8,128)} %get-tuple-element.59), channel_id=1, source_target_pairs={{0,1},{1,2},{2,3},{3,4},{4,5},{5,6},{6,7},{7,0}} | collective-permute-start | bytes 7864328 | tf_op jit(solution)/shard_map/ppermute | solution.py:50
  43.2 46.1 %collective-permute-start.3 = (bf16[2048,320]{0,1:T(8,128)(2,1)S(1)}, bf16[2048,320]{0,1:T(8,128)(2,1)}, u32[]{:S(2)}, u32[]{:S(2)}) collective-permute-start(bf16[2048,320]{0,1:T(8,128)(2,1)S(1)} %collective-permute-done.1), channel_id=1, source_target_pairs={{0,1},{1,2},{2,3},{3,4},{4,5},{5,6},{6,7},{7,0}} | collective-permute-start | bytes 3932168 | tf_op jit(solution)/shard_map/ppermute | solution.py:47
  44.6 44.7 %collective-permute-start.2 = (f32[2048]{0:T(1024)S(1)}, f32[2048]{0:T(1024)S(1)}, u32[]{:S(2)}, u32[]{:S(2)}) collective-permute-start(f32[2048]{0:T(1024)S(1)} %collective-permute-done), channel_id=1, source_target_pairs={{0,1},{1,2},{2,3},{3,4},{4,5},{5,6},{6,7},{7,0}} | collective-permute-start | bytes 24584 | tf_op jit(solution)/shard_map/ppermute | solution.py:48
  91.0 13.7 %copy-start.5 = (bf16[2048,320]{0,1:T(8,128)(2,1)S(1)}, bf16[2048,320]{0,1:T(8,128)(2,1)}, u32[]{:S(2)}) copy-start(bf16[2048,320]{0,1:T(8,128)(2,1)} %get-tuple-element.39) | copy-start | bytes 3932164 | tf_op jit(solution)/shard_map/cond
  114.0 4.6 %copy-start = (f32[2048,320]{0,1:T(8,128)}, f32[2048,320]{0,1:T(8,128)S(1)}, u32[]{:S(2)}) copy-start(f32[2048,320]{0,1:T(8,128)S(1)} %get-tuple-element.57) | copy-start | bytes 7864324
  114.0 50.7 %copy-start.7 = (f32[2048]{0:T(1024)S(1)}, f32[2048]{0:T(1024)}, u32[]{:S(2)}) copy-start(f32[2048]{0:T(1024)} %param.10) | copy-start | bytes 24580
  118.6 52.8 %collective-permute-start.7 = (f32[2048,320]{0,1:T(8,128)}, f32[2048,320]{0,1:T(8,128)}, u32[]{:S(2)}, u32[]{:S(2)}) collective-permute-start(f32[2048,320]{0,1:T(8,128)} %add.87), channel_id=1, source_target_pairs={{0,1},{1,2},{2,3},{3,4},{4,5},{5,6},{6,7},{7,0}} | collective-permute-start | bytes 7864328 | tf_op jit(solution)/shard_map/ppermute | solution.py:50
  118.6 46.1 %collective-permute-start.5 = (bf16[2048,320]{0,1:T(8,128)(2,1)}, bf16[2048,320]{0,1:T(8,128)(2,1)}, u32[]{:S(2)}, u32[]{:S(2)}) collective-permute-start(bf16[2048,320]{0,1:T(8,128)(2,1)} %collective-permute-done.3), channel_id=1, source_target_pairs={{0,1},{1,2},{2,3},{3,4},{4,5},{5,6},{6,7},{7,0}} | collective-permute-start | bytes 3932168 | tf_op jit(solution)/shard_map/ppermute | solution.py:47
  119.2 45.6 %collective-permute-start.4 = (f32[2048]{0:T(1024)S(1)}, f32[2048]{0:T(1024)S(1)}, u32[]{:S(2)}, u32[]{:S(2)}) collective-permute-start(f32[2048]{0:T(1024)S(1)} %collective-permute-done.2), channel_id=1, source_target_pairs={{0,1},{1,2},{2,3},{3,4},{4,5},{5,6},{6,7},{7,0}} | collective-permute-start | bytes 24584 | tf_op jit(solution)/shard_map/ppermute | solution.py:48
  171.4 4.6 %copy-start.2 = (f32[2048,320]{0,1:T(8,128)}, f32[2048,320]{0,1:T(8,128)S(1)}, u32[]{:S(2)}) copy-start(f32[2048,320]{0,1:T(8,128)S(1)} %get-tuple-element.58) | copy-start | bytes 7864324
  171.5 4.6 %copy-start.3 = (bf16[2048,320]{0,1:T(8,128)(2,1)S(1)}, bf16[2048,320]{0,1:T(8,128)(2,1)}, u32[]{:S(2)}) copy-start(bf16[2048,320]{0,1:T(8,128)(2,1)} %param.9) | copy-start | bytes 3932164
  176.1 91.1 %collective-permute-start.8 = (f32[2048,320]{0,1:T(8,128)}, f32[2048,320]{0,1:T(8,128)}, u32[]{:S(2)}, u32[]{:S(2)}) collective-permute-start(f32[2048,320]{0,1:T(8,128)} %add.88), channel_id=1, source_target_pairs={{0,5},{1,6},{2,7},{3,0},{4,1},{5,2},{6,3},{7,4}} | collective-permute-start | bytes 7864328 | tf_op jit(solution)/shard_map/ppermute | solution.py:56
  191.6 75.6 %copy-start.1 = (f32[2048,320]{0,1:T(8,128)S(1)}, f32[2048,320]{0,1:T(8,128)}, u32[]{:S(2)}) copy-start(f32[2048,320]{0,1:T(8,128)} %copy-done) | copy-start | bytes 7864324
where the time goes:
time: 275 us
  waiting for transfers between devices  101 us (37%)
  matrix products  68.3 us (25%)
  blocking collectives  67 us (24%)
  other arithmetic  19.6 us (7%)
  loops' own time  7.46 us (3%)
  starting transfers between devices  5.57 us (2%)
  between operations  3.77 us (1%)
    ppermute x3, waiting for transfers between devices, device_fn(): q_vis = lax.ppermute(q_vis, 'seg', fwd_perm)  101 us
    psum x1, blocking collectives, device_fn(): energy = lax.psum(energy, 'seg')  67 us
    dot_general x3, matrix products, pair_weights(): jnp.einsum('id,jd->ij', positions, x_vis, preferred_element_type=jnp.floa...  42 us
    add x2, other arithmetic, device_fn(): react_acc = react_acc + vis_part  9.15 us
    dot_general x2, matrix products, live_pair(): jnp.einsum('ij,id->jd', w_low, positions, preferred_element_type=jnp.floa...  8.87 us
    dot_general x2, matrix products, live_pair(): host_pull = jnp.dot(w_low, x_vis, preferred_element_type=jnp.float32)  8.85 us
    dot_general x1, matrix products, device_fn(): jnp.dot(self_w.astype(jnp.bfloat16), positions, preferred_element_type=jn...  8.61 us
    another operation x3, loops' own time, device_fn(): lax.cond(band_row[reach_steps - step_idx] != 0, live_pair, dead_pair, (x_...  7.46 us
  transfers between devices with their start and end apart: 9, of which 3 were waited for; matrix products, arithmetic and copies ran while one was open for 19% of the time, Pallas kernels for 0%

commit v1 on v0

v1 whole, which is shorter than its diff:
```python
import functools

import jax
import jax.numpy as jnp
from jax import lax
from jax.experimental import pallas as pl
from jax.experimental.pallas import tpu as pltpu
from jax.sharding import PartitionSpec as P

MESH = pl.DeviceIdType.MESH
LOG2E = 1.4426950408889634
CHUNK = 512
TILE = 256
PARTS = 4
ORDER = [(0, c) for c in range(4)] + [(1, c) for c in range(4)] + [
    (2, 0), (4, 0), (3, 0), (2, 1), (4, 1), (3, 1), (2, 2), (4, 2), (3, 2), (2, 3), (4, 3), (3, 3),
    (6, 0), (5, 2), (5, 0), (6, 2), (6, 1), (5, 3), (5, 1), (6, 3)]
POS = {rc: i for i, rc in enumerate(ORDER)}
N_CHUNK = len(ORDER)
FORWARDS = (
    [((2, c), 'core', (3, c)) for c in range(4)]
    + [((4, c), 'x', (6, c)) for c in range(2)]
    + [((2, c), 'y', (5, c)) for c in range(2, 4)]
    + [((6, c), 'core', (5, c)) for c in range(2)]
    + [((5, c), 'core', (6, c)) for c in range(2, 4)])
FIRSTS = [((0, c), link, (role, c)) for c in range(4) for link, role in (('x', 2), ('yo', 4), ('core', 1))]
SENDS = FIRSTS + FORWARDS


def split3(v):
    hi = v.astype(jnp.bfloat16)
    rest = v - hi.astype(jnp.float32)
    mid = rest.astype(jnp.bfloat16)
    low = (rest - mid.astype(jnp.float32)).astype(jnp.bfloat16)
    return hi.astype(jnp.float32), mid.astype(jnp.float32), low.astype(jnp.float32)


def kernel(inv_lsq, x_ref, q_ref, band_ref, out_ref, en_ref,
           xi, xj, qj, qi, s0, s1, acc, rs, bound, eslot, mpos,
           send_x, recv_x, send_q, recv_q, send_e, recv_e):
    n_rows, feat = x_ref.shape
    depth = xj.shape[1]
    n_tiles = n_rows // TILE
    scale = LOG2E * inv_lsq
    my_sys = lax.axis_index('sys')
    me = lax.axis_index('seg')
    core = lax.rem(me, 2)
    xc = lax.rem(me // 2, 2)
    yc = me // 4

    def dev(y, x, c):
        return (y * 2 + x) * 2 + c

    owner = {0: me, 1: dev(yc, xc, 1 - core), 2: dev(yc, 1 - xc, core), 3: dev(yc, 1 - xc, 1 - core),
             4: dev(1 - yc, xc, 1 - core), 5: dev(1 - yc, 1 - xc, core), 6: dev(1 - yc, 1 - xc, 1 - core)}
    target = {'core': owner[1], 'x': owner[2], 'yo': owner[4], 'y': dev(1 - yc, xc, core)}

    barrier = pltpu.get_barrier_semaphore()
    for step in range(1, 8):
        pl.semaphore_signal(barrier, inc=1, device_id=(my_sys, lax.rem(me + step, 8)), device_id_type=MESH)

    def copies(k):
        src, link, dst = SENDS[k]
        s, d = POS[src], POS[dst]
        to = (my_sys, target[link])
        return (
            pltpu.make_async_remote_copy(src_ref=qj.at[s], dst_ref=qj.at[d], send_sem=send_q.at[k],
                                         recv_sem=recv_q.at[d], device_id=to, device_id_type=MESH),
            pltpu.make_async_remote_copy(src_ref=xj.at[s], dst_ref=xj.at[d], send_sem=send_x.at[k],
                                         recv_sem=recv_x.at[d], device_id=to, device_id_type=MESH))

    def arrived(p):
        to = (my_sys, me)
        pltpu.make_async_remote_copy(src_ref=qj.at[p], dst_ref=qj.at[p], send_sem=send_q.at[0],
                                     recv_sem=recv_q.at[p], device_id=to, device_id_type=MESH).wait_recv()
        pltpu.make_async_remote_copy(src_ref=xj.at[p], dst_ref=xj.at[p], send_sem=send_x.at[0],
                                     recv_sem=recv_x.at[p], device_id=to, device_id_type=MESH).wait_recv()

    lane = lax.broadcasted_iota(jnp.int32, (128, 128), 1)
    for g in range(n_rows // 128):
        r0 = g * 128
        c, j0 = r0 // CHUNK, r0 % CHUNK
        rows = slice(r0, r0 + 128)
        x_a = x_ref[rows, 0:128]
        x_b = x_ref[rows, 128:256]
        xi[rows, 0:128] = x_a
        xi[rows, 128:256] = x_b
        xi[rows, 256:feat] = x_ref[rows, 256:feat]
        x_c = xi[rows, 256:384].astype(jnp.float32)
        x_c = jnp.where(lane < feat - 256, x_c, 0.0)
        fa, fb = x_a.astype(jnp.float32), x_b.astype(jnp.float32)
        half = -0.5 * jnp.sum(fa * fa + fb * fb + x_c * x_c, axis=1, keepdims=True)
        pieces = split3(half)
        l0 = feat - 256
        v_i = jnp.where((lane >= l0) & (lane < l0 + 3), 1.0, x_c)
        v_j = jnp.where((lane >= l0 + 3) & (lane < l0 + 6), 1.0, x_c)
        for k in range(3):
            v_i = jnp.where(lane == l0 + 3 + k, pieces[k], v_i)
            v_j = jnp.where(lane == l0 + k, pieces[k], v_j)
        xi[rows, 256:384] = v_i.astype(jnp.bfloat16)
        xj[c, 0:128, j0:j0 + 128] = x_a.T
        xj[c, 128:256, j0:j0 + 128] = x_b.T
        xj[c, 256:depth, j0:j0 + 128] = v_j.T[0:depth - 256].astype(jnp.bfloat16)
        q_row = q_ref[:, rows]
        qj[c, :, j0:j0 + 128] = q_row
        qi[rows, :] = jnp.broadcast_to(q_row, (128, 128)).T

    pl.semaphore_wait(barrier, 7)
    for k in range(len(FIRSTS)):
        for copy in copies(k):
            copy.start()

    tr = lax.broadcasted_iota(jnp.int32, (TILE, TILE), 0)
    tc = lax.broadcasted_iota(jnp.int32, (TILE, TILE), 1)
    bound[0] = jnp.zeros((TILE, TILE), jnp.float32)
    bound[1] = jnp.where(tr == tc, -1e30, 0.0)
    acc[...] = jnp.zeros_like(acc)
    rs[...] = jnp.zeros_like(rs)
    for p, (role, _) in enumerate(ORDER):
        mpos[p] = band_ref[0, lax.rem(owner[role] - me + 11, 8)].astype(jnp.float32)

    def cross(p, t, jt, s_new):
        rows, cols = slice(t * TILE, (t + 1) * TILE), slice(jt * TILE, (jt + 1) * TILE)
        s_new[jt, rows, :] = jnp.dot(xi[rows, 0:depth], xj[p, :, cols], preferred_element_type=jnp.float32)

    def phase(p_new, s_new, p_old, s_old):
        mark = None if p_old is None else mpos[p_old]
        for t in range(n_tiles):
            rows = slice(t * TILE, (t + 1) * TILE)
            row_part, pull = None, None
            for jt in range(CHUNK // TILE):
                cols = slice(jt * TILE, (jt + 1) * TILE)
                if s_new is not None:
                    cross(p_new, t, jt, s_new)
                s = s_old[jt, rows, :]
                if t % 2 == jt:
                    top = bound[jnp.where(p_old == t // 2, 1, 0)]
                else:
                    top = 0.0
                e = jnp.exp2(jnp.minimum(s, top) * scale)
                q_rows = qi[rows, :]
                w = jnp.concatenate([e[:, 0:128] * q_rows, e[:, 128:256] * q_rows], axis=1)
                w = w * (qj[p_old, :, cols] * mark)
                part = w[:, 0:128] + w[:, 128:256]
                row_part = part if row_part is None else row_part + part
                prod = lax.dot_general(xj[p_old, 0:feat, cols], w.astype(jnp.bfloat16), (((1,), (1,)), ((), ())),
                                       preferred_element_type=jnp.float32)
                pull = prod if pull is None else pull + prod
            acc[:, rows] += pull
            rs[rows, :] += row_part

    for t in range(n_tiles):
        for jt in range(CHUNK // TILE):
            cross(0, t, jt, s1)

    def pass_on(p):
        for k in range(len(FIRSTS), len(SENDS)):
            if POS[SENDS[k][0]] == p:
                for copy in copies(k):
                    copy.start()

    forward_at = sorted({POS[f[0]] for f in FORWARDS})

    def pair(i, carry):
        p1, p2 = 2 * i + 1, 2 * i + 2

        @pl.when(p1 >= PARTS)
        def _():
            arrived(p1)

        @pl.when(p2 >= PARTS)
        def _():
            arrived(p2)

        for f in sorted({(fp - 1) // 2 for fp in forward_at}):
            @pl.when(i == f)
            def _():
                for fp in forward_at:
                    if (fp - 1) // 2 == f:
                        pass_on(fp)

        phase(p1, s0, p1 - 1, s1)
        phase(p2, s1, p1, s0)
        return carry

    lax.fori_loop(0, (N_CHUNK - 2) // 2, pair, 0)
    arrived(N_CHUNK - 1)
    phase(N_CHUNK - 1, s0, N_CHUNK - 2, s1)
    phase(None, None, N_CHUNK - 1, s0)

    eslot[me] = 0.5 * jnp.sum(rs[...].reshape(n_rows // 8, 8, 128), axis=0)

    def finish(g):
        rows = slice(g * 128, (g + 1) * 128)
        total = jnp.sum(rs[rows, :], axis=1, keepdims=True)
        for k0, k1 in ((0, 128), (128, 256), (256, feat)):
            x_part = x_ref[rows, k0:k1].astype(jnp.float32)
            out_ref[rows, k0:k1] = (total * x_part - acc[k0:k1, rows].T) * inv_lsq

    def energy_copy(step):
        return pltpu.make_async_remote_copy(
            src_ref=eslot.at[me], dst_ref=eslot.at[me], send_sem=send_e.at[step - 1],
            recv_sem=recv_e.at[step - 1], device_id=(my_sys, lax.rem(me + step, 8)), device_id_type=MESH)

    for g in range(n_rows // 256):
        finish(g)
    for step in range(1, 8):
        energy_copy(step).start()
    for g in range(n_rows // 256, n_rows // 128):
        finish(g)
    for k in range(len(SENDS)):
        for copy in copies(k):
            copy.wait_send()
    for step in range(1, 8):
        energy_copy(step).wait_send()
        src = lax.rem(me - step + 8, 8)
        pltpu.make_async_remote_copy(
            src_ref=eslot.at[src], dst_ref=eslot.at[src], send_sem=send_e.at[step - 1],
            recv_sem=recv_e.at[step - 1], device_id=(my_sys, me), device_id_type=MESH).wait_recv()
    total = eslot[0]
    for d in range(1, 8):
        total = total + eslot[d]
    en_ref[...] = jnp.broadcast_to(jnp.sum(total, keepdims=True), en_ref.shape)


def solution(mesh):
    def device_fn(positions, charges, pair_band):
        n_rows, feat = positions.shape
        depth = feat + 16
        vmem = pl.BlockSpec(memory_space=pltpu.VMEM)
        f32, bf16 = jnp.float32, jnp.bfloat16
        dma = pltpu.SemaphoreType.DMA
        forces, energy = pl.pallas_call(
            functools.partial(kernel, 1.0 / feat),
            out_shape=[jax.ShapeDtypeStruct((n_rows, feat), f32), jax.ShapeDtypeStruct((8, 128), f32)],
            in_specs=[vmem, vmem, pl.BlockSpec(memory_space=pltpu.SMEM)],
            out_specs=[vmem, vmem],
            scratch_shapes=[
                pltpu.VMEM((n_rows, 384), bf16),
                pltpu.VMEM((N_CHUNK, depth, CHUNK), bf16),
                pltpu.VMEM((N_CHUNK, 1, CHUNK), f32),
                pltpu.VMEM((n_rows, 128), f32),
                pltpu.VMEM((CHUNK // TILE, n_rows, TILE), f32),
                pltpu.VMEM((CHUNK // TILE, n_rows, TILE), f32),
                pltpu.VMEM((feat, n_rows), f32),
                pltpu.VMEM((n_rows, 128), f32),
                pltpu.VMEM((2, TILE, TILE), f32),
                pltpu.VMEM((8, 8, 128), f32),
                pltpu.SMEM((N_CHUNK,), f32),
                dma((len(SENDS),)), dma((N_CHUNK,)), dma((len(SENDS),)), dma((N_CHUNK,)),
                dma((7,)), dma((7,)),
            ],
            compiler_params=pltpu.CompilerParams(
                collective_id=0, has_side_effects=True, vmem_limit_bytes=60 * 1024 * 1024),
            name='pair_forces',
        )(positions, charges.reshape(1, n_rows), pair_band)
        return forces, energy[0, 0:1]

    row_spec = P(('sys', 'seg'), None)
    vec_spec = P(('sys', 'seg'))
    return jax.shard_map(device_fn, mesh=mesh, in_specs=(row_spec, vec_spec, row_spec),
                         out_specs=(row_spec, P('sys')), check_vma=False)
```

time: 275 us -> 78.6 us (0.29)
  waiting for transfers between devices: 101 us -> 0 us
  Pallas kernels: 0 us -> 70.7 us
  matrix products: 68.3 us -> 0 us
  blocking collectives: 67 us -> 0 us
  other arithmetic: 19.6 us -> 0 us
  loops' own time: 7.46 us -> 0 us
  starting transfers between devices: 5.57 us -> 0 us
  local copies, waits for them, and re-layouts: 2 us -> 7.11 us
  between operations: 3.77 us -> 0.64 us
    ppermute x9 -> x0, waiting for transfers between devices: 101 us -> none  [the longest x3 101 us: device_fn(): q_vis = lax.ppermute(q_vis, 'seg', fwd_perm)]
    pallas_call x0 -> x1, Pallas kernels: none -> 70.7 us  [device_fn(): pl.pallas_call(functools.partial(kernel, 1.0 / feat), out_shape=[jax.Shap...]
    dot_general x8 -> x0, matrix products: 68.3 us -> none  [the longest x3 42 us: pair_weights(): jnp.einsum('id,jd->ij', positions, x_vis, preferred_element_type=jnp.floa...]
    psum x1 -> x0, blocking collectives: 67 us -> none  [device_fn(): energy = lax.psum(energy, 'seg')]
    add x3 -> x0, other arithmetic: 16.1 us -> none  [the longest x2 9.15 us: device_fn(): react_acc = react_acc + vis_part]
    another operation x3 -> x0, loops' own time: 7.46 us -> none  [device_fn(): lax.cond(band_row[reach_steps - step_idx] != 0, live_pair, dead_pair, (x_...]
    unnamed x10 -> x2, local copies, waits for them, and re-layouts: 0.03 us -> 5.93 us
    ppermute x9 -> x0, starting transfers between devices: 5.57 us -> none  [the longest x3 2.88 us: device_fn(): x_vis = lax.ppermute(x_vis, 'seg', fwd_perm)]
  transfers between devices with their start and end apart: 9 -> 0, of which waited for: 3 -> 0; matrix products, arithmetic and copies ran while one was open for 19% -> 0% of each run, Pallas kernels for 0% -> 0%
where the time goes in v1:
time: 78.6 us; the launch traced here: 78.5 us
  Pallas kernels  70.7 us (90%)
  local copies, waits for them, and re-layouts  7.11 us (9%)
    pallas_call x1, Pallas kernels, device_fn(): pl.pallas_call(functools.partial(kernel, 1.0 / feat), out_shape=[jax.Shap...  70.7 us
    unnamed x2, local copies, waits for them, and re-layouts  5.93 us

profile of v1, /device:TPU:0, one launch (start us, length us, event | category | flops | bytes accessed | tf_op | source)
XLA Modules:
  0.0 78.5 jit_solution(7385157437100916038)
XLA Ops:
  0.6 2.5 %copy.5.x_ref = bf16[2048,320]{1,0:T(8,128)(2,1)} copy(bf16[2048,320]{0,1:T(8,128)(2,1)} %param.3) | data formatting | bytes 2621440 | tf_op args[0]
  3.2 70.7 %pair_forces.1 = (f32[2048,320]{1,0:T(8,128)}, f32[8,128]{1,0:T(8,128)}) custom-call(bf16[2048,320]{1,0:T(8,128)(2,1)} %copy.5.x_ref, f32[1,2048]{1,0:T(1,128)} %bitcast.2, s32[1,7]{1,0:T(1,128)} %band_ref.1), custom_call_target="tpu_custom_call" | custom-call | tf_op jit(solution)/shard_map/pair_forces/pallas_call | solution.py:233
  73.9 1.2 %slice.3 = f32[1,1]{1,0:T(1,128)} slice(f32[8,128]{1,0:T(8,128)} %get-tuple-element.5), slice={[0:1], [0:1]} | slice | bytes 8 | tf_op jit(solution)/shard_map/slice | solution.py:257
  75.1 3.4 %copy.6 = f32[2048,320]{0,1:T(8,128)} copy(f32[2048,320]{1,0:T(8,128)} %get-tuple-element.6) | data formatting | bytes 5242880

commit v2 on v1

--- a/solution.py
+++ b/solution.py
@@ -36,9 +36,9 @@
 
 
 def kernel(inv_lsq, x_ref, q_ref, band_ref, out_ref, en_ref,
-           xi, xj, qj, qi, s0, s1, acc, rs, bound, eslot, mpos,
-           send_x, recv_x, send_q, recv_q, send_e, recv_e):
-    n_rows, feat = x_ref.shape
+           xi, xj, qj, qi, s0, s1, acc, rs, bound, eslot, mpos, aux,
+           send_x, recv_x, send_q, recv_q, send_e, recv_e, out_sem):
+    feat, n_rows = x_ref.shape
     depth = xj.shape[1]
     n_tiles = n_rows // TILE
     scale = LOG2E * inv_lsq
@@ -76,39 +76,36 @@
         pltpu.make_async_remote_copy(src_ref=xj.at[p], dst_ref=xj.at[p], send_sem=send_x.at[0],
                                      recv_sem=recv_x.at[p], device_id=to, device_id_type=MESH).wait_recv()
 
-    lane = lax.broadcasted_iota(jnp.int32, (128, 128), 1)
-    for g in range(n_rows // 128):
-        r0 = g * 128
-        c, j0 = r0 // CHUNK, r0 % CHUNK
-        rows = slice(r0, r0 + 128)
-        x_a = x_ref[rows, 0:128]
-        x_b = x_ref[rows, 128:256]
-        xi[rows, 0:128] = x_a
-        xi[rows, 128:256] = x_b
-        xi[rows, 256:feat] = x_ref[rows, 256:feat]
-        x_c = xi[rows, 256:384].astype(jnp.float32)
-        x_c = jnp.where(lane < feat - 256, x_c, 0.0)
-        fa, fb = x_a.astype(jnp.float32), x_b.astype(jnp.float32)
-        half = -0.5 * jnp.sum(fa * fa + fb * fb + x_c * x_c, axis=1, keepdims=True)
-        pieces = split3(half)
-        l0 = feat - 256
-        v_i = jnp.where((lane >= l0) & (lane < l0 + 3), 1.0, x_c)
-        v_j = jnp.where((lane >= l0 + 3) & (lane < l0 + 6), 1.0, x_c)
+    row8 = lax.broadcasted_iota(jnp.int32, (8, CHUNK), 0)
+    extra_i = []
+    for c in range(PARTS):
+        cols = slice(c * CHUNK, (c + 1) * CHUNK)
+        x_c = x_ref[:, cols]
+        xj[c, 0:feat, :] = x_c
+        x_f = x_c.astype(jnp.float32)
+        pieces = split3(-0.5 * jnp.sum(x_f * x_f, axis=0, keepdims=True))
+        v_j = jnp.where((row8 >= 3) & (row8 < 6), 1.0, 0.0)
+        v_i = jnp.where(row8 < 3, 1.0, 0.0)
         for k in range(3):
-            v_i = jnp.where(lane == l0 + 3 + k, pieces[k], v_i)
-            v_j = jnp.where(lane == l0 + k, pieces[k], v_j)
-        xi[rows, 256:384] = v_i.astype(jnp.bfloat16)
-        xj[c, 0:128, j0:j0 + 128] = x_a.T
-        xj[c, 128:256, j0:j0 + 128] = x_b.T
-        xj[c, 256:depth, j0:j0 + 128] = v_j.T[0:depth - 256].astype(jnp.bfloat16)
-        q_row = q_ref[:, rows]
-        qj[c, :, j0:j0 + 128] = q_row
-        qi[rows, :] = jnp.broadcast_to(q_row, (128, 128)).T
+            v_j = jnp.where(row8 == k, pieces[k], v_j)
+            v_i = jnp.where(row8 == 3 + k, pieces[k], v_i)
+        xj[c, feat:depth, :] = v_j.astype(jnp.bfloat16)
+        aux[:, cols] = v_i
+        qj[c] = q_ref[:, cols]
 
     pl.semaphore_wait(barrier, 7)
     for k in range(len(FIRSTS)):
         for copy in copies(k):
             copy.start()
+
+    for g in range(n_rows // 128):
+        rows = slice(g * 128, (g + 1) * 128)
+        xi[rows, 0:128] = x_ref[0:128, rows].T
+        xi[rows, 128:256] = x_ref[128:256, rows].T
+        last = jnp.concatenate([x_ref[256:feat, rows].astype(jnp.float32), aux[:, rows],
+                                jnp.zeros((384 - depth, 128), jnp.float32)], axis=0)
+        xi[rows, 256:384] = last.T.astype(jnp.bfloat16)
+        qi[rows, :] = jnp.broadcast_to(q_ref[:, rows], (128, 128)).T
 
     tr = lax.broadcasted_iota(jnp.int32, (TILE, TILE), 0)
     tc = lax.broadcasted_iota(jnp.int32, (TILE, TILE), 1)
@@ -190,24 +187,27 @@
 
     eslot[me] = 0.5 * jnp.sum(rs[...].reshape(n_rows // 8, 8, 128), axis=0)
 
-    def finish(g):
-        rows = slice(g * 128, (g + 1) * 128)
-        total = jnp.sum(rs[rows, :], axis=1, keepdims=True)
-        for k0, k1 in ((0, 128), (128, 256), (256, feat)):
-            x_part = x_ref[rows, k0:k1].astype(jnp.float32)
-            out_ref[rows, k0:k1] = (total * x_part - acc[k0:k1, rows].T) * inv_lsq
+    def out_copy(t):
+        cols = slice(t * TILE, (t + 1) * TILE)
+        return pltpu.make_async_copy(acc.at[:, cols], out_ref.at[:, cols], out_sem.at[t])
+
+    def finish(t):
+        for r0 in (t * TILE, t * TILE + 128):
+            rows = slice(r0, r0 + 128)
+            total = jnp.sum(rs[rows, :].T, axis=0, keepdims=True)
+            acc[:, rows] = (total * x_ref[:, rows].astype(jnp.float32) - acc[:, rows]) * inv_lsq
+        out_copy(t).start()
 
     def energy_copy(step):
         return pltpu.make_async_remote_copy(
             src_ref=eslot.at[me], dst_ref=eslot.at[me], send_sem=send_e.at[step - 1],
             recv_sem=recv_e.at[step - 1], device_id=(my_sys, lax.rem(me + step, 8)), device_id_type=MESH)
 
-    for g in range(n_rows // 256):
-        finish(g)
+    finish(0)
     for step in range(1, 8):
         energy_copy(step).start()
-    for g in range(n_rows // 256, n_rows // 128):
-        finish(g)
+    for t in range(1, n_tiles):
+        finish(t)
     for k in range(len(SENDS)):
         for copy in copies(k):
             copy.wait_send()
@@ -220,21 +220,23 @@
     total = eslot[0]
     for d in range(1, 8):
         total = total + eslot[d]
-    en_ref[...] = jnp.broadcast_to(jnp.sum(total, keepdims=True), en_ref.shape)
+    en_ref[0] = jnp.sum(total)
+    for t in range(n_tiles):
+        out_copy(t).wait()
 
 
 def solution(mesh):
     def device_fn(positions, charges, pair_band):
         n_rows, feat = positions.shape
-        depth = feat + 16
+        depth = feat + 8
         vmem = pl.BlockSpec(memory_space=pltpu.VMEM)
         f32, bf16 = jnp.float32, jnp.bfloat16
         dma = pltpu.SemaphoreType.DMA
         forces, energy = pl.pallas_call(
             functools.partial(kernel, 1.0 / feat),
-            out_shape=[jax.ShapeDtypeStruct((n_rows, feat), f32), jax.ShapeDtypeStruct((8, 128), f32)],
+            out_shape=[jax.ShapeDtypeStruct((feat, n_rows), f32), jax.ShapeDtypeStruct((1,), f32)],
             in_specs=[vmem, vmem, pl.BlockSpec(memory_space=pltpu.SMEM)],
-            out_specs=[vmem, vmem],
+            out_specs=[pl.BlockSpec(memory_space=pltpu.HBM), pl.BlockSpec(memory_space=pltpu.SMEM)],
             scratch_shapes=[
                 pltpu.VMEM((n_rows, 384), bf16),
                 pltpu.VMEM((N_CHUNK, depth, CHUNK), bf16),
@@ -247,14 +249,15 @@
                 pltpu.VMEM((2, TILE, TILE), f32),
                 pltpu.VMEM((8, 8, 128), f32),
                 pltpu.SMEM((N_CHUNK,), f32),
+                pltpu.VMEM((8, n_rows), f32),
                 dma((len(SENDS),)), dma((N_CHUNK,)), dma((len(SENDS),)), dma((N_CHUNK,)),
-                dma((7,)), dma((7,)),
+                dma((7,)), dma((7,)), dma((n_rows // TILE,)),
             ],
             compiler_params=pltpu.CompilerParams(
                 collective_id=0, has_side_effects=True, vmem_limit_bytes=60 * 1024 * 1024),
             name='pair_forces',
-        )(positions, charges.reshape(1, n_rows), pair_band)
-        return forces, energy[0, 0:1]
+        )(positions.T, charges.reshape(1, n_rows), pair_band)
+        return forces.T, energy
 
     row_spec = P(('sys', 'seg'), None)
     vec_spec = P(('sys', 'seg'))

time: 78.6 us -> 74.4 us (0.947)
  local copies, waits for them, and re-layouts: 7.11 us -> 3.53 us
  Pallas kernels: 70.7 us -> 68.3 us
  between operations: 0.64 us -> 2.4 us
    pallas_call x1, Pallas kernels: 70.7 us -> 68.3 us  [device_fn(): pl.pallas_call(functools.partial(kernel, 1.0 / feat), out_shape=[jax.Shap...]
    unnamed x2 -> x1, local copies, waits for them, and re-layouts: 5.93 us -> 3.53 us
    slice x1 -> x0, local copies, waits for them, and re-layouts: 1.19 us -> none  [device_fn(): return (forces, energy[0, 0:1])]
where the time goes in v2:
time: 74.4 us; the launch traced here: 74.2 us
  Pallas kernels  68.3 us (92%)
  local copies, waits for them, and re-layouts  3.53 us (5%)
  between operations  2.4 us (3%)
    pallas_call x1, Pallas kernels, device_fn(): pl.pallas_call(functools.partial(kernel, 1.0 / feat), out_shape=[jax.Shap...  68.3 us
    unnamed x1, local copies, waits for them, and re-layouts  3.53 us

profile of v2, /device:TPU:0, one launch (start us, length us, event | category | flops | bytes accessed | tf_op | source)
XLA Modules:
  0.0 74.2 jit_solution(12490085582029172052)
XLA Ops:
  0.6 68.3 %pair_forces.1 = (f32[320,2048]{1,0:T(8,128)}, f32[1]{0:T(128)}) custom-call(bf16[320,2048]{1,0:T(8,128)(2,1)} %bitcast.4, f32[1,2048]{1,0:T(1,128)} %bitcast.5, s32[1,7]{1,0:T(1,128)} %band_ref.1), custom_call_target="tpu_custom_call" | custom-call | tf_op jit(solution)/shard_map/pair_forces/pallas_call | solution.py:235
  68.9 3.5 %copy.7 = f32[2048,320]{0,1:T(8,128)} copy(f32[2048,320]{0,1:T(8,128)} %bitcast.3) | data formatting | bytes 5242880

commit v3 on v2

--- a/solution.py
+++ b/solution.py
@@ -37,7 +37,7 @@
 
 def kernel(inv_lsq, x_ref, q_ref, band_ref, out_ref, en_ref,
            xi, xj, qj, qi, s0, s1, acc, rs, bound, eslot, mpos, aux,
-           send_x, recv_x, send_q, recv_q, send_e, recv_e, out_sem):
+           send_x, recv_x, send_q, recv_q, send_e, recv_e):
     feat, n_rows = x_ref.shape
     depth = xj.shape[1]
     n_tiles = n_rows // TILE
@@ -187,16 +187,11 @@
 
     eslot[me] = 0.5 * jnp.sum(rs[...].reshape(n_rows // 8, 8, 128), axis=0)
 
-    def out_copy(t):
-        cols = slice(t * TILE, (t + 1) * TILE)
-        return pltpu.make_async_copy(acc.at[:, cols], out_ref.at[:, cols], out_sem.at[t])
-
     def finish(t):
         for r0 in (t * TILE, t * TILE + 128):
             rows = slice(r0, r0 + 128)
             total = jnp.sum(rs[rows, :].T, axis=0, keepdims=True)
-            acc[:, rows] = (total * x_ref[:, rows].astype(jnp.float32) - acc[:, rows]) * inv_lsq
-        out_copy(t).start()
+            out_ref[:, rows] = (total * x_ref[:, rows].astype(jnp.float32) - acc[:, rows]) * inv_lsq
 
     def energy_copy(step):
         return pltpu.make_async_remote_copy(
@@ -221,8 +216,6 @@
     for d in range(1, 8):
         total = total + eslot[d]
     en_ref[0] = jnp.sum(total)
-    for t in range(n_tiles):
-        out_copy(t).wait()
 
 
 def solution(mesh):
@@ -234,9 +227,9 @@
         dma = pltpu.SemaphoreType.DMA
         forces, energy = pl.pallas_call(
             functools.partial(kernel, 1.0 / feat),
-            out_shape=[jax.ShapeDtypeStruct((feat, n_rows), f32), jax.ShapeDtypeStruct((1,), f32)],
+            out_shape=[pltpu.VMEM((feat, n_rows), f32), jax.ShapeDtypeStruct((1,), f32)],
             in_specs=[vmem, vmem, pl.BlockSpec(memory_space=pltpu.SMEM)],
-            out_specs=[pl.BlockSpec(memory_space=pltpu.HBM), pl.BlockSpec(memory_space=pltpu.SMEM)],
+            out_specs=[vmem, pl.BlockSpec(memory_space=pltpu.SMEM)],
             scratch_shapes=[
                 pltpu.VMEM((n_rows, 384), bf16),
                 pltpu.VMEM((N_CHUNK, depth, CHUNK), bf16),
@@ -251,10 +244,10 @@
                 pltpu.SMEM((N_CHUNK,), f32),
                 pltpu.VMEM((8, n_rows), f32),
                 dma((len(SENDS),)), dma((N_CHUNK,)), dma((len(SENDS),)), dma((N_CHUNK,)),
-                dma((7,)), dma((7,)), dma((n_rows // TILE,)),
+                dma((7,)), dma((7,)),
             ],
             compiler_params=pltpu.CompilerParams(
-                collective_id=0, has_side_effects=True, vmem_limit_bytes=60 * 1024 * 1024),
+                collective_id=0, has_side_effects=True, vmem_limit_bytes=40 * 1024 * 1024),
             name='pair_forces',
         )(positions.T, charges.reshape(1, n_rows), pair_band)
         return forces.T, energy

time: 74.4 us -> 74.2 us (level)
  Pallas kernels: 68.3 us -> 67.5 us
    pallas_call x1, Pallas kernels: 68.3 us -> 67.5 us  [device_fn(): pl.pallas_call(functools.partial(kernel, 1.0 / feat), out_shape=[pltpu.VM...]
    unnamed x1 -> x7, local copies, waits for them, and re-layouts: 3.53 us -> 4.15 us
where the time goes in v3:
time: 74.2 us; the launch traced here: 74 us
  Pallas kernels  67.5 us (91%)
  local copies, waits for them, and re-layouts  4.15 us (6%)
  between operations  2.39 us (3%)
    pallas_call x1, Pallas kernels, device_fn(): pl.pallas_call(functools.partial(kernel, 1.0 / feat), out_shape=[pltpu.VM...  67.5 us
    unnamed x7, local copies, waits for them, and re-layouts  4.15 us

profile of v3, /device:TPU:0, one launch (start us, length us, event | category | flops | bytes accessed | tf_op | source)
XLA Modules:
  0.0 74.0 jit_solution(14545656343456853012)
XLA Ops:
  0.6 0.0 copy-start
  0.6 1.3 %copy-done = bf16[2048,320]{0,1:T(8,128)(2,1)S(1)} copy-done((bf16[2048,320]{0,1:T(8,128)(2,1)S(1)}, bf16[2048,320]{0,1:T(8,128)(2,1)}, u32[]{:S(2)}) %copy-start) | copy-done | bytes 1310744
  1.9 0.0 copy-start.1
  1.9 0.7 copy-done.1
  2.6 0.0 copy-start.2
  2.6 0.7 copy-done.2
  3.3 67.5 %pair_forces.1 = (f32[320,2048]{1,0:T(8,128)S(1)}, f32[1]{0:T(128)}) custom-call(bf16[320,2048]{1,0:T(8,128)(2,1)S(1)} %bitcast.4, f32[1,2048]{1,0:T(1,128)S(1)} %bitcast.5, s32[1,7]{1,0:T(1,128)S(1)} %copy-done.2), custom_call_target="tpu_custom_call" | custom-call | tf_op jit(solution)/shard_map/pair_forces/pallas_call | solution.py:228
  70.8 1.5 %copy.7 = f32[2048,320]{0,1:T(8,128)} copy(f32[2048,320]{0,1:T(8,128)S(1)} %bitcast.3) | data formatting | bytes 5242880
Async XLA Ops:
  0.6 1.3 %copy-start = (bf16[2048,320]{0,1:T(8,128)(2,1)S(1)}, bf16[2048,320]{0,1:T(8,128)(2,1)}, u32[]{:S(2)}) copy-start(bf16[2048,320]{0,1:T(8,128)(2,1)} %param.3) | copy-start | bytes 3932164
  1.9 0.7 copy-start.1
  2.6 0.7 copy-start.2

commit v4 on v3

v4 whole, which is shorter than its diff:
```python
import functools

import jax
import jax.numpy as jnp
from jax import lax
from jax.experimental import pallas as pl
from jax.experimental.pallas import tpu as pltpu
from jax.sharding import PartitionSpec as P

MESH = pl.DeviceIdType.MESH
LOG2E = 1.4426950408889634
CHUNK = 512
TILE = 256
PARTS = 4
ORDER = [(0, c) for c in range(4)] + [(1, c) for c in range(4)] + [
    (2, 0), (4, 0), (3, 0), (2, 1), (4, 1), (3, 1), (2, 2), (4, 2), (3, 2), (2, 3), (4, 3), (3, 3),
    (6, 0), (5, 2), (5, 0), (6, 2), (6, 1), (5, 3), (5, 1), (6, 3)]
POS = {rc: i for i, rc in enumerate(ORDER)}
N_CHUNK = len(ORDER)
FORWARDS = (
    [((2, c), 'core', (3, c)) for c in range(4)]
    + [((4, c), 'x', (6, c)) for c in range(2)]
    + [((2, c), 'y', (5, c)) for c in range(2, 4)]
    + [((6, c), 'core', (5, c)) for c in range(2)]
    + [((5, c), 'core', (6, c)) for c in range(2, 4)])
FIRSTS = [((0, c), link, (role, c)) for c in range(4) for link, role in (('x', 2), ('yo', 4), ('core', 1))]
SENDS = FIRSTS + FORWARDS


def split3(v):
    hi = v.astype(jnp.bfloat16)
    rest = v - hi.astype(jnp.float32)
    mid = rest.astype(jnp.bfloat16)
    low = (rest - mid.astype(jnp.float32)).astype(jnp.bfloat16)
    return hi.astype(jnp.float32), mid.astype(jnp.float32), low.astype(jnp.float32)


def kernel(inv_lsq, x_ref, q_ref, band_ref, out_ref, en_ref,
           xi, xj, qj, qi, s0, s1, acc, react, gift, rs, cs_own, cs_react, cs_gift, diag, eslot, band, mpos, aux,
           send_x, recv_x, send_q, recv_q, send_e, recv_e, send_g, recv_g, load_x, load_q, load_b):
    feat, n_rows = x_ref.shape
    depth = xj.shape[1]
    n_tiles = n_rows // TILE
    per_chunk = CHUNK // TILE
    scale = LOG2E * inv_lsq
    my_sys = lax.axis_index('sys')
    me = lax.axis_index('seg')
    core = lax.rem(me, 2)
    xc = lax.rem(me // 2, 2)
    yc = me // 4

    def dev(y, x, c):
        return (y * 2 + x) * 2 + c

    owner = {0: me, 1: dev(yc, xc, 1 - core), 2: dev(yc, 1 - xc, core), 3: dev(yc, 1 - xc, 1 - core),
             4: dev(1 - yc, xc, 1 - core), 5: dev(1 - yc, 1 - xc, core), 6: dev(1 - yc, 1 - xc, 1 - core)}
    target = {'core': owner[1], 'x': owner[2], 'yo': owner[4], 'y': dev(1 - yc, xc, core)}

    barrier = pltpu.get_barrier_semaphore()
    for step in range(1, 8):
        pl.semaphore_signal(barrier, inc=1, device_id=(my_sys, lax.rem(me + step, 8)), device_id_type=MESH)

    def loads(c):
        cols = slice(c * CHUNK, (c + 1) * CHUNK)
        return (pltpu.make_async_copy(x_ref.at[:, cols], xj.at[c, pl.ds(0, feat), :], load_x.at[c]),
                pltpu.make_async_copy(q_ref.at[:, cols], qj.at[c], load_q.at[c]))

    band_load = pltpu.make_async_copy(band_ref, band, load_b)
    for c in range(PARTS):
        for copy in loads(c):
            copy.start()
    band_load.start()

    def copies(k):
        src, link, dst = SENDS[k]
        s, d = POS[src], POS[dst]
        to = (my_sys, target[link])
        return (
            pltpu.make_async_remote_copy(src_ref=qj.at[s], dst_ref=qj.at[d], send_sem=send_q.at[k],
                                         recv_sem=recv_q.at[d], device_id=to, device_id_type=MESH),
            pltpu.make_async_remote_copy(src_ref=xj.at[s], dst_ref=xj.at[d], send_sem=send_x.at[k],
                                         recv_sem=recv_x.at[d], device_id=to, device_id_type=MESH))

    def arrived(p):
        to = (my_sys, me)
        pltpu.make_async_remote_copy(src_ref=qj.at[p], dst_ref=qj.at[p], send_sem=send_q.at[0],
                                     recv_sem=recv_q.at[p], device_id=to, device_id_type=MESH).wait_recv()
        pltpu.make_async_remote_copy(src_ref=xj.at[p], dst_ref=xj.at[p], send_sem=send_x.at[0],
                                     recv_sem=recv_x.at[p], device_id=to, device_id_type=MESH).wait_recv()

    row8 = lax.broadcasted_iota(jnp.int32, (8, CHUNK), 0)
    extra_i = []
    for c in range(PARTS):
        cols = slice(c * CHUNK, (c + 1) * CHUNK)
        for copy in loads(c):
            copy.wait()
        x_f = xj[c, 0:feat, :].astype(jnp.float32)
        pieces = split3(-0.5 * jnp.sum(x_f * x_f, axis=0, keepdims=True))
        v_j = jnp.where((row8 >= 3) & (row8 < 6), 1.0, 0.0)
        v_i = jnp.where(row8 < 3, 1.0, 0.0)
        for k in range(3):
            v_j = jnp.where(row8 == k, pieces[k], v_j)
            v_i = jnp.where(row8 == 3 + k, pieces[k], v_i)
        xj[c, feat:depth, :] = v_j.astype(jnp.bfloat16)
        aux[:, cols] = v_i

    pl.semaphore_wait(barrier, 7)
    for k in range(len(FIRSTS)):
        for copy in copies(k):
            copy.start()

    for g in range(n_rows // 128):
        rows = slice(g * 128, (g + 1) * 128)
        c, l0 = g * 128 // CHUNK, g * 128 % CHUNK
        cols = slice(l0, l0 + 128)
        xi[rows, 0:128] = xj[c, 0:128, cols].T
        xi[rows, 128:256] = xj[c, 128:256, cols].T
        last = jnp.concatenate([xj[c, 256:feat, cols].astype(jnp.float32), aux[:, rows],
                                jnp.zeros((384 - depth, 128), jnp.float32)], axis=0)
        xi[rows, 256:384] = last.T.astype(jnp.bfloat16)
        qi[rows, :] = jnp.broadcast_to(qj[c, :, cols], (128, 128)).T

    tr = lax.broadcasted_iota(jnp.int32, (TILE, TILE), 0)
    tc = lax.broadcasted_iota(jnp.int32, (TILE, TILE), 1)
    diag[...] = jnp.where(tr == tc, -1e30, 0.0)
    for ref in (acc, react, rs, cs_own, cs_react):
        ref[...] = jnp.zeros_like(ref)
    band_load.wait()
    for p, (role, _) in enumerate(ORDER):
        mpos[p] = band[0, lax.rem(owner[role] - me + 11, 8)].astype(jnp.float32)

    half = n_tiles // 2
    own_steps = []
    for r in (1, 2, 3):
        a2 = 4 // (r + 1)
        own_steps.append([([2 * a, 2 * a + 1], b, b * CHUNK) for a, b in ((0, r), (a2, 6 - r - a2))])
    own_diag = [([2 * c, 2 * c + 1], c, None) for c in range(PARTS)]
    peer_steps = []
    for k in range(4):
        part = lax.rem(k // 2 + core, 2) * 2 + k % 2
        tiles = list(range(k // 2 * half, (k // 2 + 1) * half))
        peer_steps.append([(tiles, PARTS + part, pl.multiple_of(part * CHUNK, CHUNK))])

    def whole(p):
        return [(list(range(n_tiles)), p, None)]

    def crosses(step, s_new):
        def one(n, t, p, jt):
            rows, cols = slice(t * TILE, (t + 1) * TILE), slice(jt * TILE, (jt + 1) * TILE)
            s_new[n] = jnp.dot(xi[rows, 0:depth], xj[p, :, cols], preferred_element_type=jnp.float32)
        todo = [(t, p, jt) for tiles, p, _ in step for t in tiles for jt in range(per_chunk)]
        return [functools.partial(one, n, *args) for n, args in enumerate(todo)]

    def consume(step, s_old, masked=False, back=None, cs=None):
        n = 0
        for tiles, p, first in step:
            mark = mpos[p]
            pulls, sums = [None] * per_chunk, [None] * per_chunk
            for ti, t in enumerate(tiles):
                rows = slice(t * TILE, (t + 1) * TILE)
                t_lane = t * TILE % CHUNK
                row_part, pull = None, None
                for jt in range(per_chunk):
                    yield
                    cols = slice(jt * TILE, (jt + 1) * TILE)
                    top = diag[...] if masked and ti == jt else 0.0
                    e = jnp.exp2(jnp.minimum(s_old[n], top) * scale)
                    q_rows = qi[rows, :]
                    w = jnp.concatenate([e[:, 0:128] * q_rows, e[:, 128:256] * q_rows], axis=1)
                    w = w * (qj[p, :, cols] * mark)
                    part = w[:, 0:128] + w[:, 128:256]
                    row_part = part if row_part is None else row_part + part
                    w_low = w.astype(jnp.bfloat16)
                    prod = lax.dot_general(xj[p, 0:feat, cols], w_low, (((1,), (1,)), ((), ())),
                                           preferred_element_type=jnp.float32)
                    pull = prod if pull is None else pull + prod
                    if back is not None:
                        prod = jnp.dot(xj[t * TILE // CHUNK, 0:feat, t_lane:t_lane + TILE], w_low,
                                       preferred_element_type=jnp.float32)
                        pulls[jt] = prod if pulls[jt] is None else pulls[jt] + prod
                        part = jnp.sum(w.reshape(TILE // 8, 8, TILE), axis=0)
                        sums[jt] = part if sums[jt] is None else sums[jt] + part
                    n += 1
                acc[:, rows] += pull
                rs[rows, :] += row_part
            if back is not None:
                for jt in range(per_chunk):
                    cols = pl.ds(first + jt * TILE, TILE)
                    back[:, cols] += pulls[jt]
                    cs[:, cols] += sums[jt]

    def phase(new, eaten, n_eaten):
        given = 0
        for k, _ in enumerate(eaten):
            upto = -(-len(new) * (k + 1) // n_eaten)
            for f in new[given:upto]:
                f()
            given = max(given, upto)

    for f in crosses(own_steps[0], s1):
        f()
    own = dict(back=acc, cs=cs_own)
    peer = dict(back=react, cs=cs_react)
    phase(crosses(own_steps[1], s0), consume(own_steps[0], s1, **own), 8)
    phase(crosses(own_steps[2], s1), consume(own_steps[1], s0, **own), 8)
    phase(crosses(own_diag, s0), consume(own_steps[2], s1, **own), 8)
    for c in range(PARTS):
        arrived(PARTS + c)
    phase(crosses(peer_steps[0], s1), consume(own_diag, s0, masked=True), 16)
    phase(crosses(peer_steps[1], s0), consume(peer_steps[0], s1, **peer), 8)
    arrived(2 * PARTS)

    def pass_on(p):
        for k in range(len(FIRSTS), len(SENDS)):
            if POS[SENDS[k][0]] == p:
                for copy in copies(k):
                    copy.start()

    pass_on(2 * PARTS)
    phase(crosses(peer_steps[2], s1), consume(peer_steps[1], s0, **peer), 8)
    phase(crosses(peer_steps[3], s0), consume(peer_steps[2], s1, **peer), 8)
    phase(crosses(whole(2 * PARTS), s1), consume(peer_steps[3], s0, **peer), 8)

    def gifts():
        to = (my_sys, owner[1])
        return (
            pltpu.make_async_remote_copy(src_ref=react, dst_ref=gift, send_sem=send_g.at[0],
                                         recv_sem=recv_g.at[0], device_id=to, device_id_type=MESH),
            pltpu.make_async_remote_copy(src_ref=cs_react, dst_ref=cs_gift, send_sem=send_g.at[1],
                                         recv_sem=recv_g.at[1], device_id=to, device_id_type=MESH))

    forward_at = sorted({POS[f[0]] for f in FORWARDS})

    def pair(i, carry):
        p1, p2 = 2 * i + 2 * PARTS + 1, 2 * i + 2 * PARTS + 2
        arrived(p1)
        arrived(p2)
        for f in range((N_CHUNK - 2 * PARTS - 2) // 2):
            due = [fp for fp in forward_at if fp - 2 * PARTS in (2 * f + 1, 2 * f + 2)]
            if due or f == 1:
                @pl.when(i == f)
                def _():
                    for fp in due:
                        pass_on(fp)
                    if f == 1:
                        for copy in gifts():
                            copy.start()

        phase(crosses(whole(p1), s0), consume(whole(p1 - 1), s1), 16)
        phase(crosses(whole(p2), s1), consume(whole(p1), s0), 16)
        return carry

    lax.fori_loop(0, (N_CHUNK - 2 * PARTS - 2) // 2, pair, 0)
    arrived(N_CHUNK - 1)
    for copy in gifts():
        copy.wait_recv()
    phase(crosses(whole(N_CHUNK - 1), s0), consume(whole(N_CHUNK - 2), s1), 16)
    phase([], consume(whole(N_CHUNK - 1), s0), 16)

    own_part = jnp.sum(rs[...].reshape(n_rows // 8, 8, 128), axis=0)
    for g in range(n_rows // 128):
        own_part = own_part + cs_own[:, g * 128:(g + 1) * 128] + cs_react[:, g * 128:(g + 1) * 128]
    eslot[me] = 0.5 * own_part

    def finish(t):
        for r0 in (t * TILE, t * TILE + 128):
            rows = slice(r0, r0 + 128)
            c, l0 = r0 // CHUNK, r0 % CHUNK
            total = jnp.sum(rs[rows, :].T, axis=0, keepdims=True)
            total = total + jnp.sum(cs_own[:, rows] + cs_gift[:, rows], axis=0, keepdims=True)
            x_part = xj[c, 0:feat, l0:l0 + 128].astype(jnp.float32)
            out_ref[:, rows] = (total * x_part - (acc[:, rows] + gift[:, rows])) * inv_lsq

    def energy_copy(step):
        return pltpu.make_async_remote_copy(
            src_ref=eslot.at[me], dst_ref=eslot.at[me], send_sem=send_e.at[step - 1],
            recv_sem=recv_e.at[step - 1], device_id=(my_sys, lax.rem(me + step, 8)), device_id_type=MESH)

    finish(0)
    for step in range(1, 8):
        energy_copy(step).start()
    for t in range(1, n_tiles):
        finish(t)
    for k in range(len(SENDS)):
        for copy in copies(k):
            copy.wait_send()
    for copy in gifts():
        copy.wait_send()
    for step in range(1, 8):
        energy_copy(step).wait_send()
        src = lax.rem(me - step + 8, 8)
        pltpu.make_async_remote_copy(
            src_ref=eslot.at[src], dst_ref=eslot.at[src], send_sem=send_e.at[step - 1],
            recv_sem=recv_e.at[step - 1], device_id=(my_sys, me), device_id_type=MESH).wait_recv()
    total = eslot[0]
    for d in range(1, 8):
        total = total + eslot[d]
    en_ref[0] = jnp.sum(total)


def solution(mesh):
    def device_fn(positions, charges, pair_band):
        n_rows, feat = positions.shape
        depth = feat + 8
        vmem = pl.BlockSpec(memory_space=pltpu.VMEM)
        hbm = pl.BlockSpec(memory_space=pltpu.HBM)
        f32, bf16 = jnp.float32, jnp.bfloat16
        dma = pltpu.SemaphoreType.DMA
        forces, energy = pl.pallas_call(
            functools.partial(kernel, 1.0 / feat),
            out_shape=[pltpu.VMEM((feat, n_rows), f32), jax.ShapeDtypeStruct((1,), f32)],
            in_specs=[hbm, hbm, hbm],
            out_specs=[vmem, pl.BlockSpec(memory_space=pltpu.SMEM)],
            scratch_shapes=[
                pltpu.VMEM((n_rows, 384), bf16),
                pltpu.VMEM((N_CHUNK, depth, CHUNK), bf16),
                pltpu.VMEM((N_CHUNK, 1, CHUNK), f32),
                pltpu.VMEM((n_rows, 128), f32),
                pltpu.VMEM((n_rows // 128, TILE, TILE), f32),
                pltpu.VMEM((n_rows // 128, TILE, TILE), f32),
                pltpu.VMEM((feat, n_rows), f32),
                pltpu.VMEM((feat, n_rows), f32),
                pltpu.VMEM((feat, n_rows), f32),
                pltpu.VMEM((n_rows, 128), f32),
                pltpu.VMEM((8, n_rows), f32),
                pltpu.VMEM((8, n_rows), f32),
                pltpu.VMEM((8, n_rows), f32),
                pltpu.VMEM((TILE, TILE), f32),
                pltpu.VMEM((8, 8, 128), f32),
                pltpu.SMEM(pair_band.shape, jnp.int32),
                pltpu.SMEM((N_CHUNK,), f32),
                pltpu.VMEM((8, n_rows), f32),
                dma((len(SENDS),)), dma((N_CHUNK,)), dma((len(SENDS),)), dma((N_CHUNK,)),
                dma((7,)), dma((7,)), dma((2,)), dma((2,)), dma((PARTS,)), dma((PARTS,)), dma,
            ],
            compiler_params=pltpu.CompilerParams(
                collective_id=0, has_side_effects=True, vmem_limit_bytes=64421888),
            name='pair_forces',
        )(positions.T, charges.reshape(1, n_rows), pair_band)
        return forces.T, energy

    row_spec = P(('sys', 'seg'), None)
    vec_spec = P(('sys', 'seg'))
    return jax.shard_map(device_fn, mesh=mesh, in_specs=(row_spec, vec_spec, row_spec),
                         out_specs=(row_spec, P('sys')), check_vma=False)
```

time: 74.2 us -> 69.8 us (0.941)
  local copies, waits for them, and re-layouts: 4.15 us -> 1.49 us
  Pallas kernels: 67.5 us -> 65.8 us
    unnamed x7 -> x1, local copies, waits for them, and re-layouts: 4.15 us -> 1.49 us
    pallas_call x1, Pallas kernels: 67.5 us -> 65.8 us  [device_fn(): pl.pallas_call(functools.partial(kernel, 1.0 / feat), out_shape=[pltpu.VM...]
where the time goes in v4:
time: 69.8 us; the launch traced here: 69.7 us
  Pallas kernels  65.8 us (94%)
  between operations  2.33 us (3%)
  local copies, waits for them, and re-layouts  1.49 us (2%)
    pallas_call x1, Pallas kernels, device_fn(): pl.pallas_call(functools.partial(kernel, 1.0 / feat), out_shape=[pltpu.VM...  65.8 us
    unnamed x1, local copies, waits for them, and re-layouts  1.49 us

profile of v4, /device:TPU:0, one launch (start us, length us, event | category | flops | bytes accessed | tf_op | source)
XLA Modules:
  0.0 69.7 jit_solution(2130959177764863825)
XLA Ops:
  0.6 65.8 %pair_forces.1 = (f32[320,2048]{1,0:T(8,128)S(1)}, f32[1]{0:T(128)}) custom-call(bf16[320,2048]{1,0:T(8,128)(2,1)} %bitcast.4, f32[1,2048]{1,0:T(1,128)} %bitcast.5, s32[1,7]{1,0:T(1,128)} %band_ref.1), custom_call_target="tpu_custom_call" | custom-call | tf_op jit(solution)/shard_map/pair_forces/pallas_call | solution.py:309
  66.5 1.5 %copy.7 = f32[2048,320]{0,1:T(8,128)} copy(f32[2048,320]{0,1:T(8,128)S(1)} %bitcast.3) | data formatting | bytes 5242880

commit v5 on v4

--- a/solution.py
+++ b/solution.py
@@ -13,8 +13,8 @@
 TILE = 256
 PARTS = 4
 ORDER = [(0, c) for c in range(4)] + [(1, c) for c in range(4)] + [
-    (2, 0), (4, 0), (3, 0), (2, 1), (4, 1), (3, 1), (2, 2), (4, 2), (3, 2), (2, 3), (4, 3), (3, 3),
-    (6, 0), (5, 2), (5, 0), (6, 2), (6, 1), (5, 3), (5, 1), (6, 3)]
+    (2, 2), (4, 0), (3, 2), (2, 3), (4, 1), (3, 3), (6, 0), (5, 2), (5, 0), (6, 2),
+    (6, 1), (5, 3), (5, 1), (6, 3), (2, 0), (4, 2), (3, 0), (2, 1), (4, 3), (3, 1)]
 POS = {rc: i for i, rc in enumerate(ORDER)}
 N_CHUNK = len(ORDER)
 FORWARDS = (
@@ -23,8 +23,10 @@
     + [((2, c), 'y', (5, c)) for c in range(2, 4)]
     + [((6, c), 'core', (5, c)) for c in range(2)]
     + [((5, c), 'core', (6, c)) for c in range(2, 4)])
-FIRSTS = [((0, c), link, (role, c)) for c in range(4) for link, role in (('x', 2), ('yo', 4), ('core', 1))]
-SENDS = FIRSTS + FORWARDS
+FIRSTS = [((0, c), link, (role, c)) for link, role, c in (
+    ('x', 2, 2), ('yo', 4, 0), ('core', 1, 0), ('x', 2, 3), ('yo', 4, 1), ('core', 1, 1), ('core', 1, 2), ('core', 1, 3))]
+LATER = [((0, c), link, (role, c)) for link, role, c in (('x', 2, 0), ('yo', 4, 2), ('x', 2, 1), ('yo', 4, 3))]
+SENDS = FIRSTS + FORWARDS + LATER
 
 
 def split3(v):
@@ -36,7 +38,7 @@
 
 
 def kernel(inv_lsq, x_ref, q_ref, band_ref, out_ref, en_ref,
-           xi, xj, qj, qi, s0, s1, acc, react, gift, rs, cs_own, cs_react, cs_gift, diag, eslot, band, mpos, aux,
+           xi, xj, qj, qi, s0, s1, acc, react, gift, rs, cs_own, cs_react, cs_gift, diag, eslot, eacc, band, mpos, epos, aux,
            send_x, recv_x, send_q, recv_q, send_e, recv_e, send_g, recv_g, load_x, load_q, load_b):
     feat, n_rows = x_ref.shape
     depth = xj.shape[1]
@@ -123,11 +125,16 @@
     tr = lax.broadcasted_iota(jnp.int32, (TILE, TILE), 0)
     tc = lax.broadcasted_iota(jnp.int32, (TILE, TILE), 1)
     diag[...] = jnp.where(tr == tc, -1e30, 0.0)
-    for ref in (acc, react, rs, cs_own, cs_react):
+    for ref in (acc, react, rs, cs_own, cs_react, eacc):
         ref[...] = jnp.zeros_like(ref)
     band_load.wait()
     for p, (role, _) in enumerate(ORDER):
         mpos[p] = band[0, lax.rem(owner[role] - me + 11, 8)].astype(jnp.float32)
+
+    on_core = core.astype(jnp.float32)
+    share = {3: 1.0 - on_core, 4: on_core}
+    for p, (role, _) in enumerate(ORDER):
+        epos[p] = share.get(role, 0.5 * jnp.ones_like(on_core))
 
     half = n_tiles // 2
     own_steps = []
@@ -151,11 +158,12 @@
         todo = [(t, p, jt) for tiles, p, _ in step for t in tiles for jt in range(per_chunk)]
         return [functools.partial(one, n, *args) for n, args in enumerate(todo)]
 
-    def consume(step, s_old, masked=False, back=None, cs=None):
+    def consume(step, s_old, masked=False, back=None, cs=None, weight=None):
         n = 0
         for tiles, p, first in step:
             mark = mpos[p]
             pulls, sums = [None] * per_chunk, [None] * per_chunk
+            e_part = jnp.zeros((8, 128), jnp.float32)
             for ti, t in enumerate(tiles):
                 rows = slice(t * TILE, (t + 1) * TILE)
                 t_lane = t * TILE % CHUNK
@@ -183,6 +191,8 @@
                     n += 1
                 acc[:, rows] += pull
                 rs[rows, :] += row_part
+                e_part = e_part + jnp.sum(row_part.reshape(TILE // 8, 8, 128), axis=0)
+            eacc[...] += e_part * (epos[p] if weight is None else weight)
             if back is not None:
                 for jt in range(per_chunk):
                     cols = pl.ds(first + jt * TILE, TILE)
@@ -199,25 +209,26 @@
 
     for f in crosses(own_steps[0], s1):
         f()
-    own = dict(back=acc, cs=cs_own)
-    peer = dict(back=react, cs=cs_react)
+    own = dict(back=acc, cs=cs_own, weight=1.0)
+    peer = dict(back=react, cs=cs_react, weight=1.0)
     phase(crosses(own_steps[1], s0), consume(own_steps[0], s1, **own), 8)
     phase(crosses(own_steps[2], s1), consume(own_steps[1], s0, **own), 8)
     phase(crosses(own_diag, s0), consume(own_steps[2], s1, **own), 8)
     for c in range(PARTS):
         arrived(PARTS + c)
-    phase(crosses(peer_steps[0], s1), consume(own_diag, s0, masked=True), 16)
+    phase(crosses(peer_steps[0], s1), consume(own_diag, s0, masked=True, weight=0.5), 16)
     phase(crosses(peer_steps[1], s0), consume(peer_steps[0], s1, **peer), 8)
-    arrived(2 * PARTS)
+    phase(crosses(peer_steps[2], s1), consume(peer_steps[1], s0, **peer), 8)
 
     def pass_on(p):
-        for k in range(len(FIRSTS), len(SENDS)):
+        for k in range(len(FIRSTS), len(FIRSTS) + len(FORWARDS)):
             if POS[SENDS[k][0]] == p:
                 for copy in copies(k):
                     copy.start()
 
-    pass_on(2 * PARTS)
-    phase(crosses(peer_steps[2], s1), consume(peer_steps[1], s0, **peer), 8)
+    for p in (2 * PARTS, 2 * PARTS + 1):
+        arrived(p)
+        pass_on(p)
     phase(crosses(peer_steps[3], s0), consume(peer_steps[2], s1, **peer), 8)
     phase(crosses(whole(2 * PARTS), s1), consume(peer_steps[3], s0, **peer), 8)
 
@@ -231,18 +242,27 @@
 
     forward_at = sorted({POS[f[0]] for f in FORWARDS})
 
+    n_pairs = (N_CHUNK - 2 * PARTS - 4) // 2
+
     def pair(i, carry):
         p1, p2 = 2 * i + 2 * PARTS + 1, 2 * i + 2 * PARTS + 2
-        arrived(p1)
+
+        @pl.when(i > 0)
+        def _():
+            arrived(p1)
+
         arrived(p2)
-        for f in range((N_CHUNK - 2 * PARTS - 2) // 2):
-            due = [fp for fp in forward_at if fp - 2 * PARTS in (2 * f + 1, 2 * f + 2)]
+        for f in range(n_pairs):
+            due = [fp for fp in forward_at if fp - 2 * PARTS in (2 * f + 1, 2 * f + 2) and fp > 2 * PARTS + 1]
             if due or f == 1:
                 @pl.when(i == f)
                 def _():
                     for fp in due:
                         pass_on(fp)
                     if f == 1:
+                        for k in range(len(FIRSTS) + len(FORWARDS), len(SENDS)):
+                            for copy in copies(k):
+                                copy.start()
                         for copy in gifts():
                             copy.start()
 
@@ -250,17 +270,18 @@
         phase(crosses(whole(p2), s1), consume(whole(p1), s0), 16)
         return carry
 
-    lax.fori_loop(0, (N_CHUNK - 2 * PARTS - 2) // 2, pair, 0)
+    lax.fori_loop(0, n_pairs, pair, 0)
+    p_late, p_end = N_CHUNK - 1 - core, N_CHUNK - 2 + core
+    arrived(N_CHUNK - 3)
+    pass_on(N_CHUNK - 3)
+    phase(crosses(whole(N_CHUNK - 3), s0), consume(whole(N_CHUNK - 4), s1), 16)
+    arrived(N_CHUNK - 2)
     arrived(N_CHUNK - 1)
     for copy in gifts():
         copy.wait_recv()
-    phase(crosses(whole(N_CHUNK - 1), s0), consume(whole(N_CHUNK - 2), s1), 16)
-    phase([], consume(whole(N_CHUNK - 1), s0), 16)
-
-    own_part = jnp.sum(rs[...].reshape(n_rows // 8, 8, 128), axis=0)
-    for g in range(n_rows // 128):
-        own_part = own_part + cs_own[:, g * 128:(g + 1) * 128] + cs_react[:, g * 128:(g + 1) * 128]
-    eslot[me] = 0.5 * own_part
+    phase(crosses(whole(p_late), s1), consume(whole(N_CHUNK - 3), s0), 16)
+    phase(crosses(whole(p_end), s0), consume(whole(p_late), s1), 16)
+    eslot[me] = eacc[...]
 
     def finish(t):
         for r0 in (t * TILE, t * TILE + 128):
@@ -276,10 +297,11 @@
             src_ref=eslot.at[me], dst_ref=eslot.at[me], send_sem=send_e.at[step - 1],
             recv_sem=recv_e.at[step - 1], device_id=(my_sys, lax.rem(me + step, 8)), device_id_type=MESH)
 
-    finish(0)
-    for step in range(1, 8):
-        energy_copy(step).start()
-    for t in range(1, n_tiles):
+    for n, _ in enumerate(consume(whole(p_end), s0)):
+        if n == 6:
+            for step in range(1, 8):
+                energy_copy(step).start()
+    for t in range(n_tiles):
         finish(t)
     for k in range(len(SENDS)):
         for copy in copies(k):
@@ -327,7 +349,9 @@
                 pltpu.VMEM((8, n_rows), f32),
                 pltpu.VMEM((TILE, TILE), f32),
                 pltpu.VMEM((8, 8, 128), f32),
+                pltpu.VMEM((8, 128), f32),
                 pltpu.SMEM(pair_band.shape, jnp.int32),
+                pltpu.SMEM((N_CHUNK,), f32),
                 pltpu.SMEM((N_CHUNK,), f32),
                 pltpu.VMEM((8, n_rows), f32),
                 dma((len(SENDS),)), dma((N_CHUNK,)), dma((len(SENDS),)), dma((N_CHUNK,)),

time: 69.8 us -> 66.6 us (0.954)
  Pallas kernels: 65.8 us -> 62.7 us
    pallas_call x1, Pallas kernels: 65.8 us -> 62.7 us  [device_fn(): pl.pallas_call(functools.partial(kernel, 1.0 / feat), out_shape=[pltpu.VM...]
where the time goes in v5:
time: 66.6 us; the launch traced here: 66.5 us
  Pallas kernels  62.7 us (94%)
  between operations  2.33 us (3%)
  local copies, waits for them, and re-layouts  1.49 us (2%)
    pallas_call x1, Pallas kernels, device_fn(): pl.pallas_call(functools.partial(kernel, 1.0 / feat), out_shape=[pltpu.VM...  62.7 us
    unnamed x1, local copies, waits for them, and re-layouts  1.49 us

profile of v5, /device:TPU:0, one launch (start us, length us, event | category | flops | bytes accessed | tf_op | source)
XLA Modules:
  0.0 66.5 jit_solution(3359512918972561032)
XLA Ops:
  0.6 62.7 %pair_forces.1 = (f32[320,2048]{1,0:T(8,128)S(1)}, f32[1]{0:T(128)}) custom-call(bf16[320,2048]{1,0:T(8,128)(2,1)} %bitcast.4, f32[1,2048]{1,0:T(1,128)} %bitcast.5, s32[1,7]{1,0:T(1,128)} %band_ref.1), custom_call_target="tpu_custom_call" | custom-call | tf_op jit(solution)/shard_map/pair_forces/pallas_call | solution.py:331
  63.3 1.5 %copy.7 = f32[2048,320]{0,1:T(8,128)} copy(f32[2048,320]{0,1:T(8,128)S(1)} %bitcast.3) | data formatting | bytes 5242880

commit v6 on v5

--- a/solution.py
+++ b/solution.py
@@ -106,6 +106,7 @@
         xj[c, feat:depth, :] = v_j.astype(jnp.bfloat16)
         aux[:, cols] = v_i
 
+    band_load.wait()
     pl.semaphore_wait(barrier, 7)
     for k in range(len(FIRSTS)):
         for copy in copies(k):
@@ -125,9 +126,8 @@
     tr = lax.broadcasted_iota(jnp.int32, (TILE, TILE), 0)
     tc = lax.broadcasted_iota(jnp.int32, (TILE, TILE), 1)
     diag[...] = jnp.where(tr == tc, -1e30, 0.0)
-    for ref in (acc, react, rs, cs_own, cs_react, eacc):
+    for ref in (rs, cs_own, eacc):
         ref[...] = jnp.zeros_like(ref)
-    band_load.wait()
     for p, (role, _) in enumerate(ORDER):
         mpos[p] = band[0, lax.rem(owner[role] - me + 11, 8)].astype(jnp.float32)
 
@@ -158,7 +158,7 @@
         todo = [(t, p, jt) for tiles, p, _ in step for t in tiles for jt in range(per_chunk)]
         return [functools.partial(one, n, *args) for n, args in enumerate(todo)]
 
-    def consume(step, s_old, masked=False, back=None, cs=None, weight=None):
+    def consume(step, s_old, masked=False, back=None, cs=None, weight=None, fresh=False, back_fresh=False, cs_fresh=False):
         n = 0
         for tiles, p, first in step:
             mark = mpos[p]
@@ -189,15 +189,15 @@
                         part = jnp.sum(w.reshape(TILE // 8, 8, TILE), axis=0)
                         sums[jt] = part if sums[jt] is None else sums[jt] + part
                     n += 1
-                acc[:, rows] += pull
+                acc[:, rows] = pull if fresh else acc[:, rows] + pull
                 rs[rows, :] += row_part
                 e_part = e_part + jnp.sum(row_part.reshape(TILE // 8, 8, 128), axis=0)
             eacc[...] += e_part * (epos[p] if weight is None else weight)
             if back is not None:
                 for jt in range(per_chunk):
                     cols = pl.ds(first + jt * TILE, TILE)
-                    back[:, cols] += pulls[jt]
-                    cs[:, cols] += sums[jt]
+                    back[:, cols] = pulls[jt] if back_fresh else back[:, cols] + pulls[jt]
+                    cs[:, cols] = sums[jt] if cs_fresh else cs[:, cols] + sums[jt]
 
     def phase(new, eaten, n_eaten):
         given = 0
@@ -210,8 +210,8 @@
     for f in crosses(own_steps[0], s1):
         f()
     own = dict(back=acc, cs=cs_own, weight=1.0)
-    peer = dict(back=react, cs=cs_react, weight=1.0)
-    phase(crosses(own_steps[1], s0), consume(own_steps[0], s1, **own), 8)
+    peer = dict(back=react, cs=cs_react, weight=1.0, back_fresh=True, cs_fresh=True)
+    phase(crosses(own_steps[1], s0), consume(own_steps[0], s1, fresh=True, back_fresh=True, **own), 8)
     phase(crosses(own_steps[2], s1), consume(own_steps[1], s0, **own), 8)
     phase(crosses(own_diag, s0), consume(own_steps[2], s1, **own), 8)
     for c in range(PARTS):
@@ -298,11 +298,12 @@
             recv_sem=recv_e.at[step - 1], device_id=(my_sys, lax.rem(me + step, 8)), device_id_type=MESH)
 
     for n, _ in enumerate(consume(whole(p_end), s0)):
-        if n == 6:
+        if n == 2:
             for step in range(1, 8):
                 energy_copy(step).start()
-    for t in range(n_tiles):
-        finish(t)
+        if n and n % 2 == 0:
+            finish(n // 2 - 1)
+    finish(n_tiles - 1)
     for k in range(len(SENDS)):
         for copy in copies(k):
             copy.wait_send()

time: 66.6 us -> 66.4 us (level)
  no operation moved by 1% of the time
where the time goes in v6:
time: 66.4 us; the launch traced here: 66.3 us
  Pallas kernels  62.5 us (94%)
  between operations  2.33 us (4%)
  local copies, waits for them, and re-layouts  1.49 us (2%)
    pallas_call x1, Pallas kernels, device_fn(): pl.pallas_call(functools.partial(kernel, 1.0 / feat), out_shape=[pltpu.VM...  62.5 us
    unnamed x1, local copies, waits for them, and re-layouts  1.49 us

profile of v6, /device:TPU:0, one launch (start us, length us, event | category | flops | bytes accessed | tf_op | source)
XLA Modules:
  0.0 66.3 jit_solution(10346843943362233043)
XLA Ops:
  0.6 62.5 %pair_forces.1 = (f32[320,2048]{1,0:T(8,128)S(1)}, f32[1]{0:T(128)}) custom-call(bf16[320,2048]{1,0:T(8,128)(2,1)} %bitcast.4, f32[1,2048]{1,0:T(1,128)} %bitcast.5, s32[1,7]{1,0:T(1,128)} %band_ref.1), custom_call_target="tpu_custom_call" | custom-call | tf_op jit(solution)/shard_map/pair_forces/pallas_call | solution.py:332
  63.1 1.5 %copy.7 = f32[2048,320]{0,1:T(8,128)} copy(f32[2048,320]{0,1:T(8,128)S(1)} %bitcast.3) | data formatting | bytes 5242880
